TPU v7x, 512 devices: a whole 4x8x8 slice. The times are simulated.
512 devices in a mesh: row: 16 (over y, core), col: 32 (over z, x).
Axes of the slice: x: 4, y: 8, z: 8, core: 2. Of those that a mesh axis runs over, the one named last changes fastest.
Arguments:
- couplings: float32 [24576, 24576], P('row', 'col'), may hold values from -0.0390625 to 0.0390625
- diag_terms: float32 [24576], P('col'), may hold values from 1 to 4
- start_block: float32 [3, 24576], P(None, 'col'), may hold values from -6 to 6
Outputs:
- basis_scaled: float32 [2, 3, 24576], P(None, None, 'col')
- coeffs: float32 [2, 2, 3, 3], replicated
All inputs are finite; a program needn't handle non-finite values.
Results may differ from a plain program's by a relative error of at most 0.0003.
Values sent between devices are 32-bit elements; how exact they have to be, the bound alone decides.
No kernel may reach another device: no remote copies, remote signals or barrier semaphores. Data moves between devices by JAX's collectives and lax.ppermute only.
A program may use at most 64 MiB of HBM per device.

v0:
```python
import jax
import jax.numpy as jnp
from jax import lax
from jax.sharding import PartitionSpec as P

ITERS = 2
M = 24576


def turned_gather(arrays, axis, dims):
    turned = [jnp.moveaxis(a, dim, 0) for a, dim in zip(arrays, dims)]
    both = jnp.concatenate([t.reshape(len(t), -1) for t in turned], axis=1)
    result, at, done = (lax.all_gather(both, axis, axis=0, tiled=True), 0, [])
    for t, dim in zip(turned, dims):
        piece = result[:, at : at + t[0].size].reshape(-1, *t.shape[1:])
        done.append(jnp.moveaxis(piece, 0, dim))
        at += t[0].size
    return tuple(done)


def from_everyone(shard, axis):
    copies = jnp.broadcast_to(shard, (lax.axis_size(axis), *shard.shape))
    return lax.all_to_all(copies, axis, split_axis=0, concat_axis=0, tiled=True)


def over_copies(shard, axis):
    everything = from_everyone(shard, axis)
    return jnp.sum(everything, axis=0)


def in_order(tiles, dim):
    shape = list(tiles.shape[1:])
    shape[dim] *= tiles.shape[0]
    return jnp.moveaxis(tiles, 0, dim).reshape(shape)


def gathered_copies(shard, axis, dim):
    return in_order(from_everyone(shard, axis), dim)


def product(a, b):
    return jnp.dot(a, b, precision=lax.Precision.HIGHEST, preferred_element_type=jnp.float32)


def product_rows(a, matrix):
    return lax.dot_general(
        a,
        matrix,
        (((1,), (1,)), ((), ())),
        precision=lax.Precision.HIGHEST,
        preferred_element_type=jnp.float32,
    )


def shards(couplings, diag_terms, start_block):
    row_index = lax.axis_index("row")
    col_index = lax.axis_index("col")
    width_row = couplings.shape[0]
    width_col = couplings.shape[1]
    root = jnp.sqrt(jnp.float32(M))
    scaled = []
    blocks = []
    start_full, diag_full = turned_gather((start_block, diag_terms), "col", (1, 0))
    first_factor = jnp.linalg.cholesky(product(start_full, start_full.T))
    current = jax.scipy.linalg.solve_triangular(first_factor, start_full, lower=True)
    basis = [current]
    for step in range(ITERS):
        col_piece = lax.dynamic_slice_in_dim(current, col_index * width_col, width_col, 1)
        row_piece = lax.dynamic_slice_in_dim(current, row_index * width_row, width_row, 1)
        forward_rows = over_copies(product_rows(col_piece, couplings), "col")
        backward_cols = over_copies(product(row_piece, couplings), "row")
        forward = lax.all_gather(forward_rows, "row", axis=1, tiled=True)
        backward = gathered_copies(backward_cols, "col", 1)
        image = diag_full[None, :] * current + 0.5 * (forward + backward)
        prior = jnp.concatenate(basis, 0)
        correlation = product(image, prior.T)
        image = image - product(correlation, prior)
        factor = jnp.linalg.cholesky(product(image, image.T))
        current = jax.scipy.linalg.solve_triangular(factor, image, lower=True)
        basis.append(current)
        own_cols = lax.dynamic_slice_in_dim(current, col_index * width_col, width_col, 1)
        scaled.append(own_cols * root)
        blocks.append(jnp.stack([correlation[:, 3 * step : 3 * step + 3], factor]))
    return (jnp.stack(scaled), jnp.stack(blocks))


def solution(mesh):
    placed = (P("row", "col"), P("col"), P(None, "col"))
    return jax.shard_map(
        shards, mesh=mesh, in_specs=placed, out_specs=(P(None, None, "col"), P()), check_vma=False
    )
```

profile of v0, /device:TPU:1, one launch (start us, length us, event | category | flops | bytes accessed | tf_op | source)
XLA Modules:
  0.0 230.9 jit_solution(8561767828042711058)
XLA Ops:
  1.3 0.7 pad_maximum_fusion.4
  2.0 44.4 %all_gather.9 = f32[24576,4]{0,1:T(4,128)S(1)} all-gather(f32[768,4]{0,1:T(4,128)S(1)} %pad_maximum_fusion.4), channel_id=1, replica_groups=mesh['row'=16,'col'=32] {'col'}, dimensions={0}, use_global_device_ids=true | all-gather | bytes 405504 | tf_op jit(solution)/shard_map/all_gather | solution.py:13
  46.5 1.8 fusion.4
  50.3 1.0 fusion.1
  51.2 4.6 %fusion.13 = f32[3,768]{1,0:T(4,128)S(1)} fusion(f32[1536,768]{1,0:T(8,128)} %param.6, f32[3,24576]{1,0:T(4,128)S(1)} %fusion.1, s32[]{:T(128)S(6)} %select_n.14), kind=kOutput, calls=%fused_computation.19 | convolution fusion | flops 42467328 | bytes 4752388 | tf_op jit(solution)/shard_map/dot_general | solution.py:42
  56.6 19.9 %all-to-all-start.1 = ((f32[16,3,768]{2,1,0:T(4,128)}), f32[16,3,768]{2,1,0:T(4,128)S(1)}, u32[]{:S(2)}, u32[]{:S(2)}) async-start(f32[16,3,768]{2,1,0:T(4,128)} %broadcast_in_dim.19), calls=%async_computation.1 | async-start | bytes 393216 | tf_op jit(solution)/shard_map/all_to_all | solution.py:23
  76.5 6.2 %fusion.15 = f32[3,1536]{1,0:T(4,128)S(1)} fusion(f32[1536,768]{1,0:T(8,128)} %param.6, f32[3,24576]{1,0:T(4,128)S(1)} %fusion.1, s32[]{:T(128)S(6)} %select_n.7), kind=kOutput, calls=%fused_computation.24 | convolution fusion | flops 42467328 | bytes 4749316 | tf_op jit(solution)/shard_map/dot_general | solution.py:46
  82.7 4.0 %all-to-all-done.1 = f32[16,3,768]{2,1,0:T(4,128)S(1)} async-done(((f32[16,3,768]{2,1,0:T(4,128)}), f32[16,3,768]{2,1,0:T(4,128)S(1)}, u32[]{:S(2)}, u32[]{:S(2)}) %all-to-all-start.1) | async-done | bytes 147488 | tf_op jit(solution)/shard_map/all_to_all | solution.py:23
  86.7 1.0 broadcast_in_dim.18
  87.7 4.9 %all-to-all-start = ((f32[32,3,1536]{2,1,0:T(4,128)}), f32[32,3,1536]{2,1,0:T(4,128)S(1)}, u32[]{:S(2)}, u32[]{:S(2)}) async-start(f32[32,3,1536]{2,1,0:T(4,128)} %broadcast_in_dim.18), calls=%async_computation | async-start | bytes 1572864 | tf_op jit(solution)/shard_map/all_to_all | solution.py:23
  92.7 22.3 %all-to-all-done = f32[32,3,1536]{2,1,0:T(4,128)S(1)} async-done(((f32[32,3,1536]{2,1,0:T(4,128)}), f32[32,3,1536]{2,1,0:T(4,128)S(1)}, u32[]{:S(2)}, u32[]{:S(2)}) %all-to-all-start) | async-done | bytes 589856 | tf_op jit(solution)/shard_map/all_to_all | solution.py:23
  115.0 0.8 broadcast_in_dim.20
  115.8 5.1 %all-to-all-start.2 = ((f32[32,3,768]{2,1,0:T(4,128)}), f32[32,3,768]{2,1,0:T(4,128)S(1)}, u32[]{:S(2)}, u32[]{:S(2)}) async-start(f32[32,3,768]{2,1,0:T(4,128)} %broadcast_in_dim.20), calls=%async_computation.2 | async-start | bytes 786432 | tf_op jit(solution)/shard_map/all_to_all | solution.py:23
  121.2 16.9 %all_gather.10 = f32[3,24576]{1,0:T(4,128)S(1)} all-gather(f32[3,1536]{1,0:T(4,128)S(1)} %reduce_sum.36), channel_id=1, replica_groups=mesh['row'=16,'col'=32] {'row'}, dimensions={1}, use_global_device_ids=true | all-gather | bytes 313344 | tf_op jit(solution)/shard_map/all_gather | solution.py:72
  138.1 1.8 fusion.6
  139.8 0.9 convolution_subtract_fusion
  140.8 1.8 fusion.41
  144.6 1.0 fusion.22
  145.5 4.6 %fusion.11 = f32[3,768]{1,0:T(4,128)S(1)} fusion(f32[1536,768]{1,0:T(8,128)} %param.6, f32[3,24576]{1,0:T(4,128)S(1)} %fusion.22, s32[]{:T(128)S(6)} %select_n.14), kind=kOutput, calls=%fused_computation.17 | convolution fusion | flops 42467328 | bytes 4752388 | tf_op jit(solution)/shard_map/dot_general | solution.py:42
  150.9 5.1 %all-to-all-start.4 = ((f32[16,3,768]{2,1,0:T(4,128)}), f32[16,3,768]{2,1,0:T(4,128)S(1)}, u32[]{:S(2)}, u32[]{:S(2)}) async-start(f32[16,3,768]{2,1,0:T(4,128)} %broadcast_in_dim.22), calls=%async_computation.4 | async-start | bytes 393216 | tf_op jit(solution)/shard_map/all_to_all | solution.py:23
  155.9 6.2 %fusion.17 = f32[3,1536]{1,0:T(4,128)S(1)} fusion(f32[1536,768]{1,0:T(8,128)} %param.6, f32[3,24576]{1,0:T(4,128)S(1)} %fusion.22, s32[]{:T(128)S(6)} %select_n.7), kind=kOutput, calls=%fused_computation.26 | convolution fusion | flops 42467328 | bytes 4749316 | tf_op jit(solution)/shard_map/dot_general | solution.py:46
  162.1 4.0 %all-to-all-done.4 = f32[16,3,768]{2,1,0:T(4,128)S(1)} async-done(((f32[16,3,768]{2,1,0:T(4,128)}), f32[16,3,768]{2,1,0:T(4,128)S(1)}, u32[]{:S(2)}, u32[]{:S(2)}) %all-to-all-start.4) | async-done | bytes 147488 | tf_op jit(solution)/shard_map/all_to_all | solution.py:23
  166.1 1.0 broadcast_in_dim.21
  167.1 9.5 %all-to-all-start.3 = ((f32[32,3,1536]{2,1,0:T(4,128)}), f32[32,3,1536]{2,1,0:T(4,128)S(1)}, u32[]{:S(2)}, u32[]{:S(2)}) async-start(f32[32,3,1536]{2,1,0:T(4,128)} %broadcast_in_dim.21), calls=%async_computation.3 | async-start | bytes 1572864 | tf_op jit(solution)/shard_map/all_to_all | solution.py:23
  176.7 22.3 %all-to-all-done.3 = f32[32,3,1536]{2,1,0:T(4,128)S(1)} async-done(((f32[32,3,1536]{2,1,0:T(4,128)}), f32[32,3,1536]{2,1,0:T(4,128)S(1)}, u32[]{:S(2)}, u32[]{:S(2)}) %all-to-all-start.3) | async-done | bytes 589856 | tf_op jit(solution)/shard_map/all_to_all | solution.py:23
  199.0 0.8 broadcast_in_dim.23
  199.8 5.1 %all-to-all-start.5 = ((f32[32,3,768]{2,1,0:T(4,128)}), f32[32,3,768]{2,1,0:T(4,128)S(1)}, u32[]{:S(2)}, u32[]{:S(2)}) async-start(f32[32,3,768]{2,1,0:T(4,128)} %broadcast_in_dim.23), calls=%async_computation.5 | async-start | bytes 786432 | tf_op jit(solution)/shard_map/all_to_all | solution.py:23
  205.1 16.9 %all_gather.11 = f32[3,24576]{1,0:T(4,128)S(1)} all-gather(f32[3,1536]{1,0:T(4,128)S(1)} %reduce_sum.38), channel_id=1, replica_groups=mesh['row'=16,'col'=32] {'row'}, dimensions={1}, use_global_device_ids=true | all-gather | bytes 313344 | tf_op jit(solution)/shard_map/all_gather | solution.py:72
  222.0 1.8 fusion
  223.8 1.0 convolution_subtract_fusion.1
  224.8 1.8 fusion.42
  228.7 1.0 fusion.20
  (40 shorter events, 9.9 us)
Async XLA Ops:
  56.6 30.1 %all-to-all-start.1 = ((f32[16,3,768]{2,1,0:T(4,128)}), f32[16,3,768]{2,1,0:T(4,128)S(1)}, u32[]{:S(2)}, u32[]{:S(2)}) async-start(f32[16,3,768]{2,1,0:T(4,128)} %broadcast_in_dim.19), calls=%async_computation.1 | async-start | bytes 393216 | tf_op jit(solution)/shard_map/all_to_all | solution.py:23
  87.7 27.3 %all-to-all-start = ((f32[32,3,1536]{2,1,0:T(4,128)}), f32[32,3,1536]{2,1,0:T(4,128)S(1)}, u32[]{:S(2)}, u32[]{:S(2)}) async-start(f32[32,3,1536]{2,1,0:T(4,128)} %broadcast_in_dim.18), calls=%async_computation | async-start | bytes 1572864 | tf_op jit(solution)/shard_map/all_to_all | solution.py:23
  115.8 22.3 %all-to-all-start.2 = ((f32[32,3,768]{2,1,0:T(4,128)}), f32[32,3,768]{2,1,0:T(4,128)S(1)}, u32[]{:S(2)}, u32[]{:S(2)}) async-start(f32[32,3,768]{2,1,0:T(4,128)} %broadcast_in_dim.20), calls=%async_computation.2 | async-start | bytes 786432 | tf_op jit(solution)/shard_map/all_to_all | solution.py:23
  150.9 15.3 %all-to-all-start.4 = ((f32[16,3,768]{2,1,0:T(4,128)}), f32[16,3,768]{2,1,0:T(4,128)S(1)}, u32[]{:S(2)}, u32[]{:S(2)}) async-start(f32[16,3,768]{2,1,0:T(4,128)} %broadcast_in_dim.22), calls=%async_computation.4 | async-start | bytes 393216 | tf_op jit(solution)/shard_map/all_to_all | solution.py:23
  167.1 31.9 %all-to-all-start.3 = ((f32[32,3,1536]{2,1,0:T(4,128)}), f32[32,3,1536]{2,1,0:T(4,128)S(1)}, u32[]{:S(2)}, u32[]{:S(2)}) async-start(f32[32,3,1536]{2,1,0:T(4,128)} %broadcast_in_dim.21), calls=%async_computation.3 | async-start | bytes 1572864 | tf_op jit(solution)/shard_map/all_to_all | solution.py:23
  199.8 22.2 %all-to-all-start.5 = ((f32[32,3,768]{2,1,0:T(4,128)}), f32[32,3,768]{2,1,0:T(4,128)S(1)}, u32[]{:S(2)}, u32[]{:S(2)}) async-start(f32[32,3,768]{2,1,0:T(4,128)} %broadcast_in_dim.23), calls=%async_computation.5 | async-start | bytes 786432 | tf_op jit(solution)/shard_map/all_to_all | solution.py:23
where the time goes:
time: 232 us; the launch traced here: 231 us
  blocking collectives  78.2 us (34%)
  waiting for transfers between devices  52.7 us (23%)
  starting transfers between devices  49.7 us (21%)
  matrix products  35.4 us (15%)
  other arithmetic  7.44 us (3%)
  local copies, waits for them, and re-layouts  6.66 us (3%)
    all_to_all x6, waiting for transfers between devices, from_everyone(): return lax.all_to_all(copies, axis, split_axis=0, concat_axis=0, tiled=True)  52.7 us
    all_to_all x6, starting transfers between devices, from_everyone(): return lax.all_to_all(copies, axis, split_axis=0, concat_axis=0, tiled=True)  49.7 us
    all_gather x1, blocking collectives, turned_gather(): result, at, done = (lax.all_gather(both, axis, axis=0, tiled=True), 0, [])  44.4 us
    all_gather x2, blocking collectives, shards(): forward = lax.all_gather(forward_rows, 'row', axis=1, tiled=True)  33.8 us
    dot_general x9, matrix products, product(): jnp.dot(a, b, precision=lax.Precision.HIGHEST, preferred_element_type=jnp...  20.2 us
    dot_general x2, matrix products, product_rows(): lax.dot_general(a, matrix, (((1,), (1,)), ((), ())), precision=lax.Precis...  12.4 us
    broadcast_in_dim x6, local copies, waits for them, and re-layouts, from_everyone(): copies = jnp.broadcast_to(shard, (lax.axis_size(axis), *shard.shape))  4.95 us
  transfers between devices with their start and end apart: 6, of which 4 were waited for; matrix products, arithmetic and copies ran while one was open for 6% of the time, Pallas kernels for 0%

commit v1 on v0

--- a/solution.py
+++ b/solution.py
@@ -69,7 +69,9 @@
         row_piece = lax.dynamic_slice_in_dim(current, row_index * width_row, width_row, 1)
         forward_rows = over_copies(product_rows(col_piece, couplings), "col")
         backward_cols = over_copies(product(row_piece, couplings), "row")
-        forward = lax.all_gather(forward_rows, "row", axis=1, tiled=True)
+        forward = jnp.concatenate(
+            lax.all_to_all(jnp.stack([forward_rows] * lax.axis_size("row")), "row", 0, 0), axis=1
+        )
         backward = gathered_copies(backward_cols, "col", 1)
         image = diag_full[None, :] * current + 0.5 * (forward + backward)
         prior = jnp.concatenate(basis, 0)

time: 232 us -> 260 us (1.12)
  waiting for transfers between devices: 52.7 us -> 107 us
  blocking collectives: 78.2 us -> 44.4 us
  starting transfers between devices: 49.7 us -> 55.2 us
    all_gather x2 -> x0, blocking collectives: 33.8 us -> none  [shards(): forward = lax.all_gather(forward_rows, 'row', axis=1, tiled=True)]
    all_to_all x0 -> x2, waiting for transfers between devices: none -> 29.1 us  [shards(): lax.all_to_all(jnp.stack([forward_rows] * lax.axis_size('row')), 'row', 0...]
    all_to_all x6, waiting for transfers between devices: 52.7 us -> 78.3 us  [from_everyone(): return lax.all_to_all(copies, axis, split_axis=0, concat_axis=0, tiled=True)]
    all_to_all x0 -> x2, starting transfers between devices: none -> 12.9 us  [shards(): lax.all_to_all(jnp.stack([forward_rows] * lax.axis_size('row')), 'row', 0...]
    all_to_all x6, starting transfers between devices: 49.7 us -> 42.3 us  [from_everyone(): return lax.all_to_all(copies, axis, split_axis=0, concat_axis=0, tiled=True)]
  transfers between devices with their start and end apart: 6 -> 8, of which waited for: 4 -> 8; matrix products, arithmetic and copies ran while one was open for 6% -> 5% of each run, Pallas kernels for 0% -> 0%
where the time goes in v1:
time: 260 us; the launch traced here: 259 us
  waiting for transfers between devices  107 us (41%)
  starting transfers between devices  55.2 us (21%)
  blocking collectives  44.4 us (17%)
  matrix products  35.4 us (14%)
  local copies, waits for them, and re-layouts  8.24 us (3%)
  other arithmetic  7.44 us (3%)
    all_to_all x6, waiting for transfers between devices, from_everyone(): return lax.all_to_all(copies, axis, split_axis=0, concat_axis=0, tiled=True)  78.3 us
    all_gather x1, blocking collectives, turned_gather(): result, at, done = (lax.all_gather(both, axis, axis=0, tiled=True), 0, [])  44.4 us
    all_to_all x6, starting transfers between devices, from_everyone(): return lax.all_to_all(copies, axis, split_axis=0, concat_axis=0, tiled=True)  42.3 us
    all_to_all x2, waiting for transfers between devices, shards(): lax.all_to_all(jnp.stack([forward_rows] * lax.axis_size('row')), 'row', 0...  29.1 us
    dot_general x9, matrix products, product(): jnp.dot(a, b, precision=lax.Precision.HIGHEST, preferred_element_type=jnp...  20.2 us
    all_to_all x2, starting transfers between devices, shards(): lax.all_to_all(jnp.stack([forward_rows] * lax.axis_size('row')), 'row', 0...  12.9 us
    dot_general x2, matrix products, product_rows(): lax.dot_general(a, matrix, (((1,), (1,)), ((), ())), precision=lax.Precis...  12.4 us
  transfers between devices with their start and end apart: 8, of which 8 were waited for; matrix products, arithmetic and copies ran while one was open for 5% of the time, Pallas kernels for 0%

profile of v1, /device:TPU:1, one launch (start us, length us, event | category | flops | bytes accessed | tf_op | source)
XLA Modules:
  0.0 258.9 jit_solution(6205729539807314754)
XLA Ops:
  2.0 44.4 %all_gather.3 = f32[24576,4]{0,1:T(4,128)S(1)} all-gather(f32[768,4]{0,1:T(4,128)S(1)} %pad_maximum_fusion.4), channel_id=1, replica_groups=mesh['row'=16,'col'=32] {'col'}, dimensions={0}, use_global_device_ids=true | all-gather | bytes 405504 | tf_op jit(solution)/shard_map/all_gather | solution.py:13
  46.5 1.8 fusion.4
  50.3 1.0 fusion.1
  51.2 4.6 %fusion.13 = f32[3,768]{1,0:T(4,128)S(1)} fusion(f32[1536,768]{1,0:T(8,128)} %param.6, f32[3,24576]{1,0:T(4,128)S(1)} %fusion.1, s32[]{:T(128)S(6)} %select_n.14), kind=kOutput, calls=%fused_computation.19 | convolution fusion | flops 42467328 | bytes 4752388 | tf_op jit(solution)/shard_map/dot_general | solution.py:42
  56.6 19.9 %all-to-all-start.2 = ((f32[16,3,768]{2,1,0:T(4,128)}), f32[16,3,768]{2,1,0:T(4,128)S(1)}, u32[]{:S(2)}, u32[]{:S(2)}) async-start(f32[16,3,768]{2,1,0:T(4,128)} %broadcast_in_dim.19), calls=%async_computation.2 | async-start | bytes 393216 | tf_op jit(solution)/shard_map/all_to_all | solution.py:23
  76.5 6.2 %fusion.15 = f32[3,1536]{1,0:T(4,128)S(1)} fusion(f32[1536,768]{1,0:T(8,128)} %param.6, f32[3,24576]{1,0:T(4,128)S(1)} %fusion.1, s32[]{:T(128)S(6)} %select_n.7), kind=kOutput, calls=%fused_computation.24 | convolution fusion | flops 42467328 | bytes 4749316 | tf_op jit(solution)/shard_map/dot_general | solution.py:46
  82.7 4.0 %all-to-all-done.2 = f32[16,3,768]{2,1,0:T(4,128)S(1)} async-done(((f32[16,3,768]{2,1,0:T(4,128)}), f32[16,3,768]{2,1,0:T(4,128)S(1)}, u32[]{:S(2)}, u32[]{:S(2)}) %all-to-all-start.2) | async-done | bytes 147488 | tf_op jit(solution)/shard_map/all_to_all | solution.py:23
  86.7 1.0 broadcast_in_dim.18
  87.7 4.9 %all-to-all-start = ((f32[32,3,1536]{2,1,0:T(4,128)}), f32[32,3,1536]{2,1,0:T(4,128)S(1)}, u32[]{:S(2)}, u32[]{:S(2)}) async-start(f32[32,3,1536]{2,1,0:T(4,128)} %broadcast_in_dim.18), calls=%async_computation | async-start | bytes 1572864 | tf_op jit(solution)/shard_map/all_to_all | solution.py:23
  92.7 22.3 %all-to-all-done = f32[32,3,1536]{2,1,0:T(4,128)S(1)} async-done(((f32[32,3,1536]{2,1,0:T(4,128)}), f32[32,3,1536]{2,1,0:T(4,128)S(1)}, u32[]{:S(2)}, u32[]{:S(2)}) %all-to-all-start) | async-done | bytes 589856 | tf_op jit(solution)/shard_map/all_to_all | solution.py:23
  115.8 5.1 %all-to-all-start.3 = ((f32[32,3,768]{2,1,0:T(4,128)}), f32[32,3,768]{2,1,0:T(4,128)S(1)}, u32[]{:S(2)}, u32[]{:S(2)}) async-start(f32[32,3,768]{2,1,0:T(4,128)} %broadcast_in_dim.20), calls=%async_computation.3 | async-start | bytes 786432 | tf_op jit(solution)/shard_map/all_to_all | solution.py:23
  121.1 13.5 %all-to-all-done.3 = f32[32,3,768]{2,1,0:T(4,128)S(1)} async-done(((f32[32,3,768]{2,1,0:T(4,128)}), f32[32,3,768]{2,1,0:T(4,128)S(1)}, u32[]{:S(2)}, u32[]{:S(2)}) %all-to-all-start.3) | async-done | bytes 294944 | tf_op jit(solution)/shard_map/all_to_all | solution.py:23
  135.3 6.1 %all-to-all-start.1 = ((f32[16,3,1536]{2,1,0:T(4,128)}), f32[16,3,1536]{2,1,0:T(4,128)S(1)}, u32[]{:S(2)}, u32[]{:S(2)}) async-start(f32[16,3,1536]{2,1,0:T(4,128)} %stack.28), calls=%async_computation.1 | async-start | bytes 786432 | tf_op jit(solution)/shard_map/all_to_all | solution.py:73
  141.6 14.5 %all-to-all-done.1 = f32[16,3,1536]{2,1,0:T(4,128)S(1)} async-done(((f32[16,3,1536]{2,1,0:T(4,128)}), f32[16,3,1536]{2,1,0:T(4,128)S(1)}, u32[]{:S(2)}, u32[]{:S(2)}) %all-to-all-start.1) | async-done | bytes 294944 | tf_op jit(solution)/shard_map/all_to_all | solution.py:73
  156.1 1.8 fusion.6
  158.8 1.8 fusion.41
  162.6 1.0 fusion.22
  163.6 4.6 %fusion.11 = f32[3,768]{1,0:T(4,128)S(1)} fusion(f32[1536,768]{1,0:T(8,128)} %param.6, f32[3,24576]{1,0:T(4,128)S(1)} %fusion.22, s32[]{:T(128)S(6)} %select_n.14), kind=kOutput, calls=%fused_computation.17 | convolution fusion | flops 42467328 | bytes 4752388 | tf_op jit(solution)/shard_map/dot_general | solution.py:42
  168.9 3.4 %all-to-all-start.6 = ((f32[16,3,768]{2,1,0:T(4,128)}), f32[16,3,768]{2,1,0:T(4,128)S(1)}, u32[]{:S(2)}, u32[]{:S(2)}) async-start(f32[16,3,768]{2,1,0:T(4,128)} %broadcast_in_dim.22), calls=%async_computation.6 | async-start | bytes 393216 | tf_op jit(solution)/shard_map/all_to_all | solution.py:23
  172.3 6.2 %fusion.17 = f32[3,1536]{1,0:T(4,128)S(1)} fusion(f32[1536,768]{1,0:T(8,128)} %param.6, f32[3,24576]{1,0:T(4,128)S(1)} %fusion.22, s32[]{:T(128)S(6)} %select_n.7), kind=kOutput, calls=%fused_computation.26 | convolution fusion | flops 42467328 | bytes 4749316 | tf_op jit(solution)/shard_map/dot_general | solution.py:46
  178.5 3.4 %all-to-all-done.6 = f32[16,3,768]{2,1,0:T(4,128)S(1)} async-done(((f32[16,3,768]{2,1,0:T(4,128)}), f32[16,3,768]{2,1,0:T(4,128)S(1)}, u32[]{:S(2)}, u32[]{:S(2)}) %all-to-all-start.6) | async-done | bytes 147488 | tf_op jit(solution)/shard_map/all_to_all | solution.py:23
  181.9 1.0 broadcast_in_dim.21
  182.9 3.9 %all-to-all-start.4 = ((f32[32,3,1536]{2,1,0:T(4,128)}), f32[32,3,1536]{2,1,0:T(4,128)S(1)}, u32[]{:S(2)}, u32[]{:S(2)}) async-start(f32[32,3,1536]{2,1,0:T(4,128)} %broadcast_in_dim.21), calls=%async_computation.4 | async-start | bytes 1572864 | tf_op jit(solution)/shard_map/all_to_all | solution.py:23
  186.9 22.3 %all-to-all-done.4 = f32[32,3,1536]{2,1,0:T(4,128)S(1)} async-done(((f32[32,3,1536]{2,1,0:T(4,128)}), f32[32,3,1536]{2,1,0:T(4,128)S(1)}, u32[]{:S(2)}, u32[]{:S(2)}) %all-to-all-start.4) | async-done | bytes 589856 | tf_op jit(solution)/shard_map/all_to_all | solution.py:23
  209.9 5.0 %all-to-all-start.7 = ((f32[32,3,768]{2,1,0:T(4,128)}), f32[32,3,768]{2,1,0:T(4,128)S(1)}, u32[]{:S(2)}, u32[]{:S(2)}) async-start(f32[32,3,768]{2,1,0:T(4,128)} %broadcast_in_dim.23), calls=%async_computation.7 | async-start | bytes 786432 | tf_op jit(solution)/shard_map/all_to_all | solution.py:23
  215.1 12.8 %all-to-all-done.7 = f32[32,3,768]{2,1,0:T(4,128)S(1)} async-done(((f32[32,3,768]{2,1,0:T(4,128)}), f32[32,3,768]{2,1,0:T(4,128)S(1)}, u32[]{:S(2)}, u32[]{:S(2)}) %all-to-all-start.7) | async-done | bytes 294944 | tf_op jit(solution)/shard_map/all_to_all | solution.py:23
  228.7 6.7 %all-to-all-start.5 = ((f32[16,3,1536]{2,1,0:T(4,128)}), f32[16,3,1536]{2,1,0:T(4,128)S(1)}, u32[]{:S(2)}, u32[]{:S(2)}) async-start(f32[16,3,1536]{2,1,0:T(4,128)} %stack.30), calls=%async_computation.5 | async-start | bytes 786432 | tf_op jit(solution)/shard_map/all_to_all | solution.py:73
  235.5 14.6 %all-to-all-done.5 = f32[16,3,1536]{2,1,0:T(4,128)S(1)} async-done(((f32[16,3,1536]{2,1,0:T(4,128)}), f32[16,3,1536]{2,1,0:T(4,128)S(1)}, u32[]{:S(2)}, u32[]{:S(2)}) %all-to-all-start.5) | async-done | bytes 294944 | tf_op jit(solution)/shard_map/all_to_all | solution.py:73
  250.0 1.8 fusion
  251.8 1.0 convolution_subtract_fusion.1
  252.8 1.8 fusion.42
  256.7 1.0 fusion.20
  (44 shorter events, 14.6 us)
Async XLA Ops:
  56.6 30.1 %all-to-all-start.2 = ((f32[16,3,768]{2,1,0:T(4,128)}), f32[16,3,768]{2,1,0:T(4,128)S(1)}, u32[]{:S(2)}, u32[]{:S(2)}) async-start(f32[16,3,768]{2,1,0:T(4,128)} %broadcast_in_dim.19), calls=%async_computation.2 | async-start | bytes 393216 | tf_op jit(solution)/shard_map/all_to_all | solution.py:23
  87.7 27.3 %all-to-all-start = ((f32[32,3,1536]{2,1,0:T(4,128)}), f32[32,3,1536]{2,1,0:T(4,128)S(1)}, u32[]{:S(2)}, u32[]{:S(2)}) async-start(f32[32,3,1536]{2,1,0:T(4,128)} %broadcast_in_dim.18), calls=%async_computation | async-start | bytes 1572864 | tf_op jit(solution)/shard_map/all_to_all | solution.py:23
  115.8 18.8 %all-to-all-start.3 = ((f32[32,3,768]{2,1,0:T(4,128)}), f32[32,3,768]{2,1,0:T(4,128)S(1)}, u32[]{:S(2)}, u32[]{:S(2)}) async-start(f32[32,3,768]{2,1,0:T(4,128)} %broadcast_in_dim.20), calls=%async_computation.3 | async-start | bytes 786432 | tf_op jit(solution)/shard_map/all_to_all | solution.py:23
  135.3 20.8 %all-to-all-start.1 = ((f32[16,3,1536]{2,1,0:T(4,128)}), f32[16,3,1536]{2,1,0:T(4,128)S(1)}, u32[]{:S(2)}, u32[]{:S(2)}) async-start(f32[16,3,1536]{2,1,0:T(4,128)} %stack.28), calls=%async_computation.1 | async-start | bytes 786432 | tf_op jit(solution)/shard_map/all_to_all | solution.py:73
  168.9 13.0 %all-to-all-start.6 = ((f32[16,3,768]{2,1,0:T(4,128)}), f32[16,3,768]{2,1,0:T(4,128)S(1)}, u32[]{:S(2)}, u32[]{:S(2)}) async-start(f32[16,3,768]{2,1,0:T(4,128)} %broadcast_in_dim.22), calls=%async_computation.6 | async-start | bytes 393216 | tf_op jit(solution)/shard_map/all_to_all | solution.py:23
  182.9 26.2 %all-to-all-start.4 = ((f32[32,3,1536]{2,1,0:T(4,128)}), f32[32,3,1536]{2,1,0:T(4,128)S(1)}, u32[]{:S(2)}, u32[]{:S(2)}) async-start(f32[32,3,1536]{2,1,0:T(4,128)} %broadcast_in_dim.21), calls=%async_computation.4 | async-start | bytes 1572864 | tf_op jit(solution)/shard_map/all_to_all | solution.py:23
  209.9 18.0 %all-to-all-start.7 = ((f32[32,3,768]{2,1,0:T(4,128)}), f32[32,3,768]{2,1,0:T(4,128)S(1)}, u32[]{:S(2)}, u32[]{:S(2)}) async-start(f32[32,3,768]{2,1,0:T(4,128)} %broadcast_in_dim.23), calls=%async_computation.7 | async-start | bytes 786432 | tf_op jit(solution)/shard_map/all_to_all | solution.py:23
  228.7 21.3 %all-to-all-start.5 = ((f32[16,3,1536]{2,1,0:T(4,128)}), f32[16,3,1536]{2,1,0:T(4,128)S(1)}, u32[]{:S(2)}, u32[]{:S(2)}) async-start(f32[16,3,1536]{2,1,0:T(4,128)} %stack.30), calls=%async_computation.5 | async-start | bytes 786432 | tf_op jit(solution)/shard_map/all_to_all | solution.py:73
